TPU v7x, 32 devices: a whole 2x2x4 slice. The times are simulated.
32 devices in a mesh: segment: 4 (over y, core), dp: 8 (over z, x).
Axes of the slice: x: 2, y: 2, z: 4, core: 2. Of those that a mesh axis runs over, the one named last changes fastest.
Arguments:
- token_ids: int32 [1024], P('dp'), may hold values from 0 to 38015, as said below
- table: bfloat16 [4752, 28672], P('segment', 'dp'), may hold values from -6 to 6
- out_grad: bfloat16 [1024, 3584], P('dp', 'segment'), may hold values from -6 to 6
Outputs:
- embedded: bfloat16 [1024, 3584], P('dp')
- table_grad: bfloat16 [4752, 28672], P('segment', 'dp')
Inputs may be any that keep to these rules, and one draw needn't show every extreme that they name: `token_ids`: in the 128 tokens of each data group, at most 16 ids lie in one segment's slice of 9504 rows with one residue modulo 8; in every data group some segment and residue has exactly 16.
All inputs are finite; a program needn't handle non-finite values.
Results may differ from a plain program's by a relative error of at most 0.001.
Values may be sent and summed in bfloat16 or wider, within the bound.
A program may use at most 64 MiB of HBM per device.

v0:
```python
import jax
import jax.numpy as jnp
from jax import lax
from jax.sharding import PartitionSpec as P

D = 3584
PACK = 8


def body(token_ids, table, out_grad):
    lines = table.shape[0]
    width = table.shape[1]
    groups = lax.axis_size("dp")
    tok_rows = token_ids.shape[0]
    quarters = D // width
    slot = lax.axis_index("dp") // quarters
    first = lax.axis_index("segment") * lines * PACK
    every_id = lax.all_gather(token_ids, "dp", axis=0, tiled=True)
    local = every_id - first
    in_section = (local >= 0) & (local < lines * PACK)
    owned = in_section & (local % PACK == slot)
    line_idx = jnp.clip(local // PACK, 0, lines - 1)
    whole_grad = lax.all_gather(out_grad, "segment", axis=1, tiled=True)
    capacity = tok_rows // PACK
    owned_grid = owned.reshape(groups, tok_rows)
    rank = jnp.cumsum(owned_grid.astype(jnp.int32), axis=1) - 1
    place = jnp.where(owned_grid, rank, capacity)
    group_rows = jnp.broadcast_to(jnp.arange(groups, dtype=jnp.int32)[:, None], (groups, tok_rows))
    row_of = (
        jnp.zeros((groups, capacity), jnp.int32)
        .at[group_rows, place]
        .set(line_idx.reshape(groups, tok_rows), mode="drop")
    )
    filled = jnp.zeros((groups, capacity), jnp.bool_).at[group_rows, place].set(True, mode="drop")
    fetched = jnp.take(table, row_of.reshape(-1), axis=0).reshape(groups, capacity, width)
    fetched = jnp.where(filled[:, :, None], fetched, jnp.zeros((), jnp.bfloat16))
    arrived = lax.all_to_all(fetched, "dp", split_axis=0, concat_axis=0, tiled=True)
    my_local = token_ids - first
    my_in = (my_local >= 0) & (my_local < lines * PACK)
    my_slot = my_local % PACK
    slot_hits = (my_slot[:, None] == jnp.arange(PACK, dtype=jnp.int32)[None, :]) & my_in[:, None]
    slot_ranks = jnp.cumsum(slot_hits.astype(jnp.int32), axis=0) - 1
    my_rank = jnp.sum(jnp.where(slot_hits, slot_ranks, 0), axis=1)
    sources = my_slot[:, None] * quarters + jnp.arange(quarters, dtype=jnp.int32)[None, :]
    flat_index = jnp.clip(sources * capacity + my_rank[:, None], 0, groups * capacity - 1)
    gathered = jnp.take(
        arrived.reshape(groups * capacity, width), flat_index.reshape(-1), axis=0
    ).reshape(tok_rows, D)
    segment_part = jnp.where(my_in[:, None], gathered.astype(jnp.float32), 0.0)
    slot_place = jnp.where(my_in, my_slot, PACK)
    token_at = (
        jnp.zeros((PACK, capacity), jnp.int32)
        .at[slot_place, my_rank]
        .set(jnp.arange(tok_rows, dtype=jnp.int32), mode="drop")
    )
    valid = jnp.zeros((PACK, capacity), jnp.bool_).at[slot_place, my_rank].set(True, mode="drop")
    grad_pick = jnp.take(whole_grad, token_at.reshape(-1), axis=0).reshape(
        PACK, capacity, quarters, width
    )
    grad_pick = jnp.where(valid[:, :, None, None], grad_pick, jnp.zeros((), jnp.bfloat16))
    grad_send = grad_pick.transpose(0, 2, 1, 3).reshape(groups, capacity, width)
    returned = lax.all_to_all(grad_send, "dp", split_axis=0, concat_axis=0, tiled=True)
    target = jnp.where(filled, row_of, lines)
    accum = (
        jnp.zeros((lines, width), jnp.float32)
        .at[target.reshape(-1)]
        .add(returned.reshape(-1, width).astype(jnp.float32), mode="drop")
    )
    embedded = lax.psum(segment_part.astype(jnp.bfloat16), "segment")
    return (embedded, accum.astype(jnp.bfloat16))


def solution(mesh):
    placed = (P("dp"), P("segment", "dp"), P("dp", "segment"))
    return jax.shard_map(
        body,
        mesh=mesh,
        in_specs=placed,
        out_specs=(P("dp", None), P("segment", "dp")),
        check_vma=False,
    )
```

profile of v0, /device:TPU:0, one launch (start us, length us, event | category | flops | bytes accessed | tf_op | source)
XLA Modules:
  0.0 159.1 jit_solution(7434590179938538914)
XLA Ops:
  7.2 22.6 %all-gather = s32[8,1,128]{2,1,0:T(1,128)S(1)} all-gather(s32[1,1,128]{2,1,0:T(1,128)} %bitcast.39), channel_id=1, replica_groups=mesh['segment'=4,'dp'=8] {'dp'}, dimensions={0}, use_global_device_ids=true | all-gather | bytes 4608 | tf_op jit(solution)/shard_map/all_gather | solution.py:18
  29.8 0.3 copy.12
  30.1 0.3 copy.13
  30.4 23.6 %compare_select_fusion = s32[8,128,1]{2,0,1:T(8,128)S(1)} fusion(pred[8,128,1]{2,0,1:T(8,128)(4,1)S(1)} %copy.13, s32[8,128,1]{2,0,1:T(8,128)S(1)} %copy.12), kind=kOutput, calls=%fused_computation.12 | output fusion | flops 135168 | bytes 9216 | tf_op jit(solution)/shard_map/jit(cumsum)/reduce_window_sum | solution.py:26
  54.0 0.2 copy.14
  54.2 0.8 multiply_reduce_fusion
  55.0 0.1 copy.19
  55.1 0.7 and_reduce_fusion
  55.8 0.1 copy.18
  56.0 4.3 %scatter_custom_fusion.4 = s32[128]{0:T(128)S(1)} fusion(s32[1024]{0:T(1024)S(1)} %bitcast.40, s32[1024]{0:T(1024)S(1)} %fusion.6, s32[]{:T(128)} %constant.70.clone.1), kind=kCustom, calls=%fused_computation.66 | custom fusion | bytes 516
  60.4 4.3 %scatter_custom_fusion.3 = pred[128]{0:T(512)(128)(4,1)S(1)} fusion(s32[1024]{0:T(1024)S(1)} %bitcast.41, pred[1024]{0:T(1024)(128)(4,1)S(1)} %broadcast.224, pred[]{:T(512)} %constant.71.clone.1), kind=kCustom, calls=%fused_computation.56 | custom fusion | bytes 129
  64.8 0.1 reshape.185
  64.9 6.6 %gather_fusion = bf16[128,3584]{1,0:T(8,128)(2,1)S(1)} fusion(bf16[1188,3584]{1,0:T(8,128)(2,1)} %param.6, s32[1024]{0:T(1024)S(1)} %pad_clamp_fusion.2), kind=kCustom, calls=%fused_computation.2 | custom fusion | bytes 1835520 | tf_op jit(solution)/shard_map/jit(_take)/gather | solution.py:35
  71.4 1.1 select_select_fusion
  72.6 3.6 %all-to-all-start = ((bf16[8,16,3584]{2,1,0:T(8,128)(2,1)}), bf16[8,16,3584]{2,1,0:T(8,128)(2,1)S(1)}, u32[]{:S(2)}, u32[]{:S(2)}) async-start(bf16[8,16,3584]{2,1,0:T(8,128)(2,1)} %select_select_fusion), calls=%async_computation | async-start | bytes 1835008 | tf_op jit(solution)/shard_map/all_to_all | solution.py:37
  76.2 0.1 fusion.4
  76.3 0.2 reduce_window_sum.23
  76.4 0.2 select_reduce_fusion
  76.7 6.4 %scatter_fusion.1 = s32[8,16]{1,0:T(8,128)S(1)} fusion(s32[8,16]{1,0:T(8,128)S(1)} %broadcast.169, s32[128]{0:T(128)S(1)} %fusion.18, s32[128]{0:T(128)S(1)} %iota.14), kind=kCustom, calls=%fused_computation.4 | custom fusion | bytes 2560 | tf_op jit(solution)/shard_map/scatter | solution.py:54
  83.0 0.1 reshape.180
  83.2 9.5 %all_gather.7 = bf16[128,3584]{1,0:T(8,128)(2,1)S(1)} all-gather(bf16[128,896]{1,0:T(8,128)(2,1)S(1)} %copy-done), channel_id=1, replica_groups=mesh['segment'=4,'dp'=8] {'segment'}, dimensions={1}, use_global_device_ids=true | all-gather | bytes 1146880 | tf_op jit(solution)/shard_map/all_gather | solution.py:23
  92.7 1.1 gather_fusion.2
  93.8 6.5 %scatter_fusion = pred[8,16]{1,0:T(8,128)(4,1)S(1)} fusion(pred[8,16]{1,0:T(8,128)(4,1)S(1)} %broadcast.166, s32[128]{0:T(128)S(1)} %fusion.18, pred[128]{0:T(512)(128)(4,1)S(1)} %broadcast.225), kind=kCustom, calls=%fused_computation.3 | custom fusion | bytes 1408 | tf_op jit(solution)/shard_map/scatter | solution.py:56
  100.3 0.2 broadcast_select_fusion
  100.5 1.1 broadcast_select_fusion.1
  101.5 5.9 %all-to-all-start.1 = ((bf16[8,16,3584]{2,1,0:T(8,128)(2,1)}), bf16[8,16,3584]{2,1,0:T(8,128)(2,1)S(1)}, u32[]{:S(2)}, u32[]{:S(2)}) async-start(bf16[8,16,3584]{2,1,0:T(8,128)(2,1)} %broadcast_select_fusion.1), calls=%async_computation.1 | async-start | bytes 1835008 | tf_op jit(solution)/shard_map/all_to_all | solution.py:62
  107.5 1.1 gather_fusion.1
  108.7 1.3 select_convert_fusion
  110.1 20.9 %all-to-all-done.1 = bf16[8,16,3584]{2,1,0:T(8,128)(2,1)S(1)} async-done(((bf16[8,16,3584]{2,1,0:T(8,128)(2,1)}), bf16[8,16,3584]{2,1,0:T(8,128)(2,1)S(1)}, u32[]{:S(2)}, u32[]{:S(2)}) %all-to-all-start.1) | async-done | bytes 917536 | tf_op jit(solution)/shard_map/all_to_all | solution.py:62
  130.9 10.0 %scatter_custom_fusion.2 = f32[1188,3584]{1,0:T(8,128)} fusion(s32[128]{0:T(128)S(1)} %fusion.16, f32[]{:T(128)} %constant.121.clone.1, bf16[128,3584]{1,0:T(8,128)(2,1)S(1)} %bitcast.35), kind=kCustom, calls=%fused_computation.8 | custom fusion | flops 917504 | bytes 17948676 | tf_op jit(solution)/shard_map/scatter-add | solution.py:67
  140.9 9.1 %convert_element_type.32 = bf16[1188,3584]{1,0:T(8,128)(2,1)} convert(f32[1188,3584]{1,0:T(8,128)} %scatter_custom_fusion.2) | non-fusion elementwise | flops 4257792 | bytes 25546752 | tf_op jit(solution)/shard_map/convert_element_type | solution.py:70
  150.1 2.2 %copy.23 = bf16[128,3584]{1,0:T(8,128)(2,1)} copy(bf16[128,3584]{1,0:T(8,128)(2,1)} %all-reduce.2.cloned.1.call-done) | data formatting | bytes 1835008
  (34 shorter events, 0.5 us)
Async XLA Ops:
  7.2 69.0 %copy-start.1 = (s32[128]{0:T(128)S(1)}, s32[128]{0:T(128)}, u32[]{:S(2)}) copy-start(s32[128]{0:T(128)} %param.5) | copy-start | bytes 1540
  7.2 76.0 %copy-start = (bf16[128,896]{1,0:T(8,128)(2,1)S(1)}, bf16[128,896]{1,0:T(8,128)(2,1)}, u32[]{:S(2)}) copy-start(bf16[128,896]{1,0:T(8,128)(2,1)} %param.7) | copy-start | bytes 688132
  72.6 29.0 %all-to-all-start = ((bf16[8,16,3584]{2,1,0:T(8,128)(2,1)}), bf16[8,16,3584]{2,1,0:T(8,128)(2,1)S(1)}, u32[]{:S(2)}, u32[]{:S(2)}) async-start(bf16[8,16,3584]{2,1,0:T(8,128)(2,1)} %select_select_fusion), calls=%async_computation | async-start | bytes 1835008 | tf_op jit(solution)/shard_map/all_to_all | solution.py:37
  101.5 29.4 %all-to-all-start.1 = ((bf16[8,16,3584]{2,1,0:T(8,128)(2,1)}), bf16[8,16,3584]{2,1,0:T(8,128)(2,1)S(1)}, u32[]{:S(2)}, u32[]{:S(2)}) async-start(bf16[8,16,3584]{2,1,0:T(8,128)(2,1)} %broadcast_select_fusion.1), calls=%async_computation.1 | async-start | bytes 1835008 | tf_op jit(solution)/shard_map/all_to_all | solution.py:62
  107.5 42.6 %all-reduce.2.cloned.1.call-start = ((), (), s32[]{:S(2)}) async-start(), calls=%async_computation.2 | async-start | bytes 1835008 | tf_op jit(solution)/shard_map/psum | solution.py:69
Sparse Core Ops, SparseCore 0:
  111.2 36.2 all-reduce.1
where the time goes:
time: 159 us
  other arithmetic  48.5 us (31%)
  local copies, waits for them, and re-layouts  33.8 us (21%)
  blocking collectives  32.1 us (20%)
  waiting for transfers between devices  20.9 us (13%)
  between operations  14.3 us (9%)
  starting transfers between devices  9.52 us (6%)
    another operation x1, other arithmetic, body(): rank = jnp.cumsum(owned_grid.astype(jnp.int32), axis=1) - 1  23.6 us
    all_gather x1, blocking collectives, body(): every_id = lax.all_gather(token_ids, 'dp', axis=0, tiled=True)  22.6 us
    all_to_all x1, waiting for transfers between devices, body(): lax.all_to_all(grad_send, 'dp', split_axis=0, concat_axis=0, tiled=True)  20.9 us
    unnamed x11, local copies, waits for them, and re-layouts  11.1 us
    scatter-add x1, other arithmetic, body(): accum = jnp.zeros((lines, width), jnp.float32).at[target.reshape(-1)].add...  10 us
    all_gather x1, blocking collectives, body(): whole_grad = lax.all_gather(out_grad, 'segment', axis=1, tiled=True)  9.52 us
    convert_element_type x1, other arithmetic, body(): return (embedded, accum.astype(jnp.bfloat16))  9.14 us
    gather x1, local copies, waits for them, and re-layouts, body(): jnp.take(table, row_of.reshape(-1), axis=0).reshape(groups, capacity, width)  6.55 us
  transfers between devices with their start and end apart: 3, of which 1 were waited for; matrix products, arithmetic and copies ran while one was open for 24% of the time, Pallas kernels for 0%

commit v1 on v0

--- a/solution.py
+++ b/solution.py
@@ -5,6 +5,27 @@
 
 D = 3584
 PACK = 8
+
+
+def in_order(parts, dim):
+    lengths = list(parts.shape[1:])
+    lengths[dim] *= parts.shape[0]
+    return jnp.moveaxis(parts, 0, dim).reshape(lengths)
+
+
+def grow_blocks(x, axis):
+    size, index = (lax.axis_size(axis), lax.axis_index(axis))
+    blocks, distance = (x[None], 1)
+    while distance < size:
+        other = lax.ppermute(blocks, axis, [(i, i ^ distance) for i in range(size)])
+        low = index & distance == 0
+        blocks = jnp.concatenate([jnp.where(low, blocks, other), jnp.where(low, other, blocks)])
+        distance *= 2
+    return blocks
+
+
+def doubled_up(x, axis, dim):
+    return in_order(grow_blocks(x, axis), dim)
 
 
 def body(token_ids, table, out_grad):
@@ -20,7 +41,7 @@
     in_section = (local >= 0) & (local < lines * PACK)
     owned = in_section & (local % PACK == slot)
     line_idx = jnp.clip(local // PACK, 0, lines - 1)
-    whole_grad = lax.all_gather(out_grad, "segment", axis=1, tiled=True)
+    whole_grad = doubled_up(out_grad, "segment", 1)
     capacity = tok_rows // PACK
     owned_grid = owned.reshape(groups, tok_rows)
     rank = jnp.cumsum(owned_grid.astype(jnp.int32), axis=1) - 1

time: 159 us -> 158 us (level)
  blocking collectives: 32.1 us -> 22 us
  waiting for transfers between devices: 20.9 us -> 26.8 us
  starting transfers between devices: 9.52 us -> 11.4 us
    all_gather x1 -> x0, blocking collectives: 9.52 us -> none  [body(): whole_grad = lax.all_gather(out_grad, 'segment', axis=1, tiled=True)]
    ppermute x0 -> x2, waiting for transfers between devices: none -> 7.61 us  [grow_blocks(): other = lax.ppermute(blocks, axis, [(i, i ^ distance) for i in range(size)])]
    all_to_all x1, waiting for transfers between devices: 20.9 us -> 16.3 us  [body(): lax.all_to_all(grad_send, 'dp', split_axis=0, concat_axis=0, tiled=True)]
    psum x1, waiting for transfers between devices: 0.01 us -> 2.81 us  [body(): embedded = lax.psum(segment_part.astype(jnp.bfloat16), 'segment')]
    ppermute x0 -> x2, starting transfers between devices: none -> 2.15 us  [grow_blocks(): other = lax.ppermute(blocks, axis, [(i, i ^ distance) for i in range(size)])]
  transfers between devices with their start and end apart: 3 -> 5, of which waited for: 1 -> 3; matrix products, arithmetic and copies ran while one was open for 24% -> 51% of each run, Pallas kernels for 0% -> 0%
where the time goes in v1:
time: 158 us; the launch traced here: 157 us
  other arithmetic  48.9 us (31%)
  local copies, waits for them, and re-layouts  33.9 us (21%)
  waiting for transfers between devices  26.8 us (17%)
  blocking collectives  22 us (14%)
  between operations  14.3 us (9%)
  starting transfers between devices  11.4 us (7%)
    another operation x1, other arithmetic, body(): rank = jnp.cumsum(owned_grid.astype(jnp.int32), axis=1) - 1  23.6 us
    all_gather x1, blocking collectives, body(): every_id = lax.all_gather(token_ids, 'dp', axis=0, tiled=True)  22 us
    all_to_all x1, waiting for transfers between devices, body(): lax.all_to_all(grad_send, 'dp', split_axis=0, concat_axis=0, tiled=True)  16.3 us
    unnamed x11, local copies, waits for them, and re-layouts  11.1 us
    scatter-add x1, other arithmetic, body(): accum = jnp.zeros((lines, width), jnp.float32).at[target.reshape(-1)].add...  9.95 us
    convert_element_type x1, other arithmetic, body(): return (embedded, accum.astype(jnp.bfloat16))  9.27 us
    ppermute x2, waiting for transfers between devices, grow_blocks(): other = lax.ppermute(blocks, axis, [(i, i ^ distance) for i in range(size)])  7.61 us
    gather x1, local copies, waits for them, and re-layouts, body(): jnp.take(table, row_of.reshape(-1), axis=0).reshape(groups, capacity, width)  6.55 us
  transfers between devices with their start and end apart: 5, of which 3 were waited for; matrix products, arithmetic and copies ran while one was open for 51% of the time, Pallas kernels for 0%

profile of v1, /device:TPU:0, one launch (start us, length us, event | category | flops | bytes accessed | tf_op | source)
XLA Modules:
  0.0 157.2 jit_solution(17998725026225555937)
XLA Ops:
  7.2 0.6 collective-permute-start
  7.7 22.0 %all-gather = s32[8,1,128]{2,1,0:T(1,128)S(1)} all-gather(s32[1,1,128]{2,1,0:T(1,128)} %bitcast.48), channel_id=1, replica_groups=mesh['segment'=4,'dp'=8] {'dp'}, dimensions={0}, use_global_device_ids=true | all-gather | bytes 4608 | tf_op jit(solution)/shard_map/all_gather | solution.py:39
  29.7 0.3 copy.15
  30.0 0.3 copy.16
  30.3 23.6 %compare_select_fusion = s32[8,128,1]{2,0,1:T(8,128)S(1)} fusion(pred[8,128,1]{2,0,1:T(8,128)(4,1)S(1)} %copy.16, s32[8,128,1]{2,0,1:T(8,128)S(1)} %copy.15), kind=kOutput, calls=%fused_computation.12 | output fusion | flops 135168 | bytes 9216 | tf_op jit(solution)/shard_map/jit(cumsum)/reduce_window_sum | solution.py:47
  54.0 0.2 copy.17
  54.2 0.8 multiply_reduce_fusion
  54.9 0.1 copy.23
  55.0 0.7 and_reduce_fusion
  55.8 0.1 copy.22
  55.9 4.3 %scatter_custom_fusion.4 = s32[128]{0:T(128)S(1)} fusion(s32[1024]{0:T(1024)S(1)} %bitcast.49, s32[1024]{0:T(1024)S(1)} %fusion.6, s32[]{:T(128)} %constant.70.clone.1), kind=kCustom, calls=%fused_computation.72 | custom fusion | bytes 516
  60.4 4.3 %scatter_custom_fusion.3 = pred[128]{0:T(512)(128)(4,1)S(1)} fusion(s32[1024]{0:T(1024)S(1)} %bitcast.50, pred[1024]{0:T(1024)(128)(4,1)S(1)} %broadcast.224, pred[]{:T(512)} %constant.71.clone.1), kind=kCustom, calls=%fused_computation.62 | custom fusion | bytes 129
  64.8 6.6 %gather_fusion = bf16[128,3584]{1,0:T(8,128)(2,1)S(1)} fusion(bf16[1188,3584]{1,0:T(8,128)(2,1)} %param.6, s32[1024]{0:T(1024)S(1)} %pad_clamp_fusion.2), kind=kCustom, calls=%fused_computation.2 | custom fusion | bytes 1835520 | tf_op jit(solution)/shard_map/jit(_take)/gather | solution.py:56
  71.4 1.1 select_select_fusion
  72.5 3.7 %all-to-all-start = ((bf16[8,16,3584]{2,1,0:T(8,128)(2,1)}), bf16[8,16,3584]{2,1,0:T(8,128)(2,1)S(1)}, u32[]{:S(2)}, u32[]{:S(2)}) async-start(bf16[8,16,3584]{2,1,0:T(8,128)(2,1)} %select_select_fusion), calls=%async_computation | async-start | bytes 1835008 | tf_op jit(solution)/shard_map/all_to_all | solution.py:58
  76.4 0.2 reduce_window_sum.23
  76.6 0.2 select_reduce_fusion
  76.8 6.4 %scatter_fusion.1 = s32[8,16]{1,0:T(8,128)S(1)} fusion(s32[8,16]{1,0:T(8,128)S(1)} %broadcast.169, s32[128]{0:T(128)S(1)} %fusion.18, s32[128]{0:T(128)S(1)} %iota.14), kind=kCustom, calls=%fused_computation.4 | custom fusion | bytes 2560 | tf_op jit(solution)/shard_map/scatter | solution.py:75
  83.3 6.5 %scatter_fusion = pred[8,16]{1,0:T(8,128)(4,1)S(1)} fusion(pred[8,16]{1,0:T(8,128)(4,1)S(1)} %broadcast.166, s32[128]{0:T(128)S(1)} %fusion.18, pred[128]{0:T(512)(128)(4,1)S(1)} %broadcast.225), kind=kCustom, calls=%fused_computation.3 | custom fusion | bytes 1408 | tf_op jit(solution)/shard_map/scatter | solution.py:77
  89.9 1.6 %collective-permute-start.1 = (bf16[2,128,896]{2,1,0:T(8,128)(2,1)S(1)}, bf16[2,128,896]{2,1,0:T(8,128)(2,1)S(1)}, u32[]{:S(2)}, u32[]{:S(2)}) collective-permute-start(bf16[2,128,896]{2,1,0:T(8,128)(2,1)S(1)} %pad_maximum_fusion), channel_id=1, source_target_pairs={{0,16},{8,24},{16,0},{24,8},{1,17},{9,25},{17,1},{25,9},{2,18},{10... | collective-permute-start | bytes 1376264 | tf_op jit(solution)/shard_map/ppermute | solution.py:20
  91.5 7.6 %collective-permute-done.1 = bf16[2,128,896]{2,1,0:T(8,128)(2,1)S(1)} collective-permute-done((bf16[2,128,896]{2,1,0:T(8,128)(2,1)S(1)}, bf16[2,128,896]{2,1,0:T(8,128)(2,1)S(1)}, u32[]{:S(2)}, u32[]{:S(2)}) %collective-permute-start.1) | collective-permute-done | bytes 458784 | tf_op jit(solution)/shard_map/ppermute | solution.py:20
  99.4 1.1 gather_fusion.2
  100.5 0.2 broadcast_select_fusion
  100.7 1.1 broadcast_select_fusion.1
  101.8 5.4 %all-to-all-start.1 = ((bf16[8,16,3584]{2,1,0:T(8,128)(2,1)}), bf16[8,16,3584]{2,1,0:T(8,128)(2,1)S(1)}, u32[]{:S(2)}, u32[]{:S(2)}) async-start(bf16[8,16,3584]{2,1,0:T(8,128)(2,1)} %broadcast_select_fusion.1), calls=%async_computation.1 | async-start | bytes 1835008 | tf_op jit(solution)/shard_map/all_to_all | solution.py:83
  107.3 1.1 gather_fusion.1
  108.4 1.3 select_convert_fusion
  109.8 16.3 %all-to-all-done.1 = bf16[8,16,3584]{2,1,0:T(8,128)(2,1)S(1)} async-done(((bf16[8,16,3584]{2,1,0:T(8,128)(2,1)}), bf16[8,16,3584]{2,1,0:T(8,128)(2,1)S(1)}, u32[]{:S(2)}, u32[]{:S(2)}) %all-to-all-start.1) | async-done | bytes 917536 | tf_op jit(solution)/shard_map/all_to_all | solution.py:83
  126.1 10.0 %scatter_custom_fusion.2 = f32[1188,3584]{1,0:T(8,128)} fusion(s32[128]{0:T(128)S(1)} %fusion.16, f32[]{:T(128)} %constant.122.clone.1, bf16[128,3584]{1,0:T(8,128)(2,1)S(1)} %bitcast.43), kind=kCustom, calls=%fused_computation.8 | custom fusion | flops 917504 | bytes 17948676 | tf_op jit(solution)/shard_map/scatter-add | solution.py:88
  136.1 9.3 %convert_element_type.32 = bf16[1188,3584]{1,0:T(8,128)(2,1)} convert(f32[1188,3584]{1,0:T(8,128)} %scatter_custom_fusion.2) | non-fusion elementwise | flops 4257792 | bytes 25546752 | tf_op jit(solution)/shard_map/convert_element_type | solution.py:91
  145.3 2.8 %all-reduce.2.cloned.1.call-done = bf16[128,3584]{1,0:T(8,128)(2,1)} async-done(((bf16[128,3584]{1,0:T(8,128)(2,1)}), bf16[128,3584]{1,0:T(8,128)(2,1)}) %all-reduce.2.cloned.1.call-update) | async-done | bytes 917520 | tf_op jit(solution)/shard_map/psum | solution.py:90
  148.1 2.2 %copy.28 = bf16[128,3584]{1,0:T(8,128)(2,1)} copy(bf16[128,3584]{1,0:T(8,128)(2,1)} %all-reduce.2.cloned.1.call-done) | data formatting | bytes 1835008
  (42 shorter events, 1.1 us)
Async XLA Ops:
  7.2 69.1 %copy-start.1 = (s32[128]{0:T(128)S(1)}, s32[128]{0:T(128)}, u32[]{:S(2)}) copy-start(s32[128]{0:T(128)} %param.5) | copy-start | bytes 1540
  7.2 82.6 %collective-permute-start = (bf16[1,128,896]{2,1,0:T(8,128)(2,1)}, bf16[1,128,896]{2,1,0:T(8,128)(2,1)S(1)}, u32[]{:S(2)}, u32[]{:S(2)}) collective-permute-start(bf16[1,128,896]{2,1,0:T(8,128)(2,1)} %bitcast.44), channel_id=1, source_target_pairs={{0,8},{8,0},{16,24},{24,16},{1,9},{9,1},{17,25},{25,17},{2,10},{10... | collective-permute-start | bytes 688136 | tf_op jit(solution)/shard_map/ppermute | solution.py:20
  29.7 60.0 %copy-start = (bf16[128,896]{1,0:T(8,128)(2,1)S(1)}, bf16[128,896]{1,0:T(8,128)(2,1)}, u32[]{:S(2)}) copy-start(bf16[128,896]{1,0:T(8,128)(2,1)} %param.7) | copy-start | bytes 688132
  72.5 29.2 %all-to-all-start = ((bf16[8,16,3584]{2,1,0:T(8,128)(2,1)}), bf16[8,16,3584]{2,1,0:T(8,128)(2,1)S(1)}, u32[]{:S(2)}, u32[]{:S(2)}) async-start(bf16[8,16,3584]{2,1,0:T(8,128)(2,1)} %select_select_fusion), calls=%async_computation | async-start | bytes 1835008 | tf_op jit(solution)/shard_map/all_to_all | solution.py:58
  89.9 9.2 %collective-permute-start.1 = (bf16[2,128,896]{2,1,0:T(8,128)(2,1)S(1)}, bf16[2,128,896]{2,1,0:T(8,128)(2,1)S(1)}, u32[]{:S(2)}, u32[]{:S(2)}) collective-permute-start(bf16[2,128,896]{2,1,0:T(8,128)(2,1)S(1)} %pad_maximum_fusion), channel_id=1, source_target_pairs={{0,16},{8,24},{16,0},{24,8},{1,17},{9,25},{17,1},{25,9},{2,18},{10... | collective-permute-start | bytes 1376264 | tf_op jit(solution)/shard_map/ppermute | solution.py:20
  101.8 24.4 %all-to-all-start.1 = ((bf16[8,16,3584]{2,1,0:T(8,128)(2,1)}), bf16[8,16,3584]{2,1,0:T(8,128)(2,1)S(1)}, u32[]{:S(2)}, u32[]{:S(2)}) async-start(bf16[8,16,3584]{2,1,0:T(8,128)(2,1)} %broadcast_select_fusion.1), calls=%async_computation.1 | async-start | bytes 1835008 | tf_op jit(solution)/shard_map/all_to_all | solution.py:83
  107.2 40.9 %all-reduce.2.cloned.1.call-start = ((), (), s32[]{:S(2)}) async-start(), calls=%async_computation.2 | async-start | bytes 1835008 | tf_op jit(solution)/shard_map/psum | solution.py:90
Sparse Core Ops, SparseCore 0:
  111.0 37.1 all-reduce.1
